TPU v7x, 128 devices: a whole 4x4x4 slice. The times are simulated.
128 devices in a mesh: node: 16 (over z, x), expert: 8 (over y, core).
Axes of the slice: x: 4, y: 4, z: 4, core: 2. Of those that a mesh axis runs over, the one named last changes fastest.
Arguments:
- tokens: bfloat16 [65536, 1024], P(('node', 'expert')), may hold values from -6 to 6
- queries: bfloat16 [65536, 1024], P(('node', 'expert')), may hold values from -6 to 6
- keys: bfloat16 [65536, 1024], P(('node', 'expert')), may hold values from -6 to 6
- values: bfloat16 [65536, 1024], P(('node', 'expert')), may hold values from -12 to 12
- neighbours: int32 [512, 8], P(('node', 'expert')), may hold values from 0 to 511, as said below
- live_bits: int32 [512, 8], P(('node', 'expert')), may hold values from 0 to 1, as said below
- out_proj: bfloat16 [1024, 1024], replicated, may hold values from -0.1875 to 0.1875
- norm_gain: float32 [1024], replicated, may hold values from 0.5 to 1.5
- router: bfloat16 [1024, 128], replicated, may hold values from -0.1875 to 0.1875
- expert: int32 [65536], P(('node', 'expert')), may hold values from 0 to 127, as said below
- slot: int32 [65536], P(('node', 'expert')), may hold values from 0 to 7, as said below
- w_up: bfloat16 [128, 1024, 4096], P(('node', 'expert')), may hold values from -0.1875 to 0.1875
- w_down: bfloat16 [128, 4096, 1024], P(('node', 'expert')), may hold values from -0.09375 to 0.09375
Outputs:
- layer_out: bfloat16 [65536, 1024], P(('node', 'expert'))
Inputs may be any that keep to these rules, and one draw needn't show every extreme that they name: Tile g is held by device g // 4 in node-major order. neighbours[g, 0] is g itself; every listed tile is held by g's device or by the device one step before or after it along node with the same expert index (wrapping around); entry 1 is always one step before and entry 2 one step after. `live_bits`: entry 0 of every row is 1. Within the 512 tokens of one device, no two tokens share both expert and slot; some expert takes all 8 slots of every device. See expert: pairs (expert, slot) are distinct within one device's tokens.
All inputs are finite; a program needn't handle non-finite values.
Results may differ from a plain program's by a relative error of at most 0.0049.
Values may be sent and summed in bfloat16 or wider, within the bound.
A program may use at most 192 MiB of HBM per device.

v0:
```python
import jax
import jax.numpy as jnp
from jax import lax
from jax.sharding import PartitionSpec as P

D = 1024
HEADS = 16
HEAD_DIM = 64
TILE = 128
NB = 8


score_scale = 0.125


def extended(shard, sides, width):
    for axis, dim in sides:
        size, length = (lax.axis_size(axis), shard.shape[dim])
        up = [(i, (i + 1) % size) for i in range(size)]
        down = [(j, i) for i, j in up]
        last = lax.slice_in_dim(shard, length - width, length, axis=dim)
        leading = lax.slice_in_dim(shard, 0, width, axis=dim)
        before = lax.ppermute(last, axis, up)
        after = lax.ppermute(leading, axis, down)
        shard = jnp.concatenate([before, shard, after], axis=dim)
    return shard


def shards(
    tokens,
    queries,
    keys,
    values,
    neighbours,
    live_bits,
    out_proj,
    norm_gain,
    router,
    expert,
    slot,
    w_up,
    w_down,
):
    tok_dev = tokens.shape[0]
    tiles_dev = tok_dev // TILE
    experts = router.shape[1]
    cap = 2 * tok_dev // experts
    both = jnp.concatenate([keys, values], axis=1)
    widened = extended(both, (("node", 0),), tok_dev)
    window_tiles = widened.reshape(3 * tiles_dev, TILE, 2 * D)
    my_node = lax.axis_index("node")
    node_count = lax.axis_size("node")
    column_count = lax.axis_size("expert")
    owner_node = neighbours // tiles_dev // column_count
    offset = (owner_node - my_node + node_count) % node_count
    block_of = jnp.where(offset == 0, 1, jnp.where(offset == 1, 2, 0))
    position = block_of * tiles_dev + neighbours % tiles_dev
    gathered = window_tiles[position]
    near_keys = gathered[..., :D].reshape(tiles_dev, NB * TILE, HEADS, HEAD_DIM)
    near_values = gathered[..., D:].reshape(tiles_dev, NB * TILE, HEADS, HEAD_DIM)
    query_tiles = queries.reshape(tiles_dev, TILE, HEADS, HEAD_DIM)
    scores = (
        jnp.einsum("tqhd,tkhd->thqk", query_tiles, near_keys, preferred_element_type=jnp.float32)
        * score_scale
    )
    visible = jnp.repeat(live_bits, TILE, axis=1) > 0
    masked = jnp.where(visible[:, None, None, :], scores, -jnp.inf)
    peak = jnp.max(masked, axis=-1, keepdims=True)
    weights = jnp.exp(masked - peak)
    weights = (weights / jnp.sum(weights, axis=-1, keepdims=True)).astype(jnp.bfloat16)
    mixed = jnp.einsum("thqk,tkhd->tqhd", weights, near_values, preferred_element_type=jnp.float32)
    attn = mixed.reshape(tok_dev, D).astype(jnp.bfloat16)
    hidden = tokens.astype(jnp.float32) + jnp.dot(
        attn, out_proj, preferred_element_type=jnp.float32
    )
    spread = jnp.mean(hidden * hidden, axis=-1, keepdims=True)
    normed = (hidden * lax.rsqrt(spread + 1e-06) * norm_gain[None, :]).astype(jnp.bfloat16)
    logits = jnp.dot(normed, router, preferred_element_type=jnp.float32)
    columns = lax.iota(jnp.int32, experts)
    chosen = jnp.sum(jnp.where(columns[None, :] == expert[:, None], logits, 0.0), axis=-1)
    gate = jax.nn.sigmoid(chosen)
    slot_cell = expert * cap + slot
    one_hot = (lax.iota(jnp.int32, experts * cap)[:, None] == slot_cell[None, :]).astype(
        jnp.bfloat16
    )
    outgoing = jnp.dot(one_hot, normed, preferred_element_type=jnp.float32).astype(jnp.bfloat16)
    up_matrix = w_up[0]
    down_matrix = w_down[0]
    block = lax.all_to_all(
        outgoing.reshape(experts, 1, cap, D),
        ("node", "expert"),
        split_axis=0,
        concat_axis=1,
        tiled=True,
    )
    token_rows = block.reshape(-1, D)
    lifted = jnp.dot(token_rows, up_matrix, preferred_element_type=jnp.float32)
    lifted = jax.nn.gelu(lifted, approximate=True).astype(jnp.bfloat16)
    result = jnp.dot(lifted, down_matrix, preferred_element_type=jnp.float32).astype(jnp.bfloat16)
    returned = lax.all_to_all(
        result.reshape(block.shape), ("node", "expert"), split_axis=1, concat_axis=0, tiled=True
    )
    flat_back = returned.reshape(experts * cap, D)
    expert_out = jnp.einsum("ct,cd->td", one_hot, flat_back, preferred_element_type=jnp.float32)
    layer_out = hidden + gate[:, None] * expert_out
    return layer_out.astype(jnp.bfloat16)


def solution(mesh):
    in_specs = (
        P(("node", "expert"), None),
        P(("node", "expert"), None),
        P(("node", "expert"), None),
        P(("node", "expert"), None),
        P(("node", "expert"), None),
        P(("node", "expert"), None),
        P(),
        P(),
        P(),
        P(("node", "expert")),
        P(("node", "expert")),
        P(("node", "expert"), None, None),
        P(("node", "expert"), None, None),
    )
    out_specs = P(("node", "expert"), None)
    return jax.shard_map(shards, mesh=mesh, in_specs=in_specs, out_specs=out_specs, check_vma=False)
```

profile of v0, /device:TPU:1, one launch (start us, length us, event | category | flops | bytes accessed | tf_op | source)
XLA Modules:
  0.0 282.7 jit_solution(710855097893655783)
XLA Ops:
  0.0 0.0 copy-start
  0.0 2.4 constant_dynamic-update-slice_fusion.1
  2.4 2.3 constant_dynamic-update-slice_fusion
  4.8 6.8 %collective-permute-start.1 = (bf16[512,2048]{1,0:T(8,128)(2,1)}, bf16[512,2048]{1,0:T(8,128)(2,1)}, u32[]{:S(2)}, u32[]{:S(2)}) collective-permute-start(bf16[512,2048]{1,0:T(8,128)(2,1)} %constant_dynamic-update-slice_fusion), channel_id=1, source_target_pairs={{8,0},{16,8},{24,16},{32,24},{40,32},{48,40},{56,48},{64,56},{72,6... | collective-permute-start | bytes 6291464 | tf_op jit(solution)/shard_map/ppermute | solution.py:24
  11.5 0.0 collective-permute-start
  11.5 0.7 compare_select_fusion
  12.2 0.1 reshape.71
  12.3 0.7 broadcast_compare_fusion
  13.0 0.1 broadcast_bitcast_fusion
  13.1 4.1 %reshape.79 = bf16[4,128,16,64]{3,2,1,0:T(8,128)(2,1)} reshape(bf16[512,1024]{1,0:T(8,128)(2,1)} %param.14) | data formatting | bytes 2097152 | tf_op jit(solution)/shard_map/reshape | solution.py:61
  17.2 0.7 multiply_add_fusion
  17.9 38.3 %collective-permute-done.1 = bf16[512,2048]{1,0:T(8,128)(2,1)} collective-permute-done((bf16[512,2048]{1,0:T(8,128)(2,1)}, bf16[512,2048]{1,0:T(8,128)(2,1)}, u32[]{:S(2)}, u32[]{:S(2)}) %collective-permute-start.1) | collective-permute-done | bytes 2097184 | tf_op jit(solution)/shard_map/ppermute | solution.py:24
  56.2 5.2 %collective-permute-done = bf16[512,2048]{1,0:T(8,128)(2,1)} collective-permute-done((bf16[512,2048]{1,0:T(8,128)(2,1)}, bf16[512,2048]{1,0:T(8,128)(2,1)}, u32[]{:S(2)}, u32[]{:S(2)}) %collective-permute-start) | collective-permute-done | bytes 2097184 | tf_op jit(solution)/shard_map/ppermute | solution.py:23
  61.4 5.9 %pad_maximum_fusion = bf16[1536,2048]{1,0:T(8,128)(2,1)} fusion(bf16[512,2048]{1,0:T(8,128)(2,1)} %collective-permute-done.1, bf16[512,2048]{1,0:T(8,128)(2,1)} %constant_dynamic-update-slice_fusion, bf16[512,2048]{1,0:T(8,128)(2,1)} %collective-permute-done), kind=kLoop, calls=%fused_computation.28 | loop fusion | flops 18874368 | bytes 12582912 | tf_op jit(solution)/shard_map/concatenate | solution.py:25
  67.3 10.0 %gather_fusion = bf16[32,128,2048]{2,1,0:T(8,128)(2,1)} fusion(bf16[12,128,2048]{2,1,0:T(8,128)(2,1)} %bitcast.66, s32[1024]{0:T(1024)S(1)} %pad_clamp_fusion), kind=kCustom, calls=%fused_computation | custom fusion | bytes 33554560 | tf_op jit(solution)/shard_map/gather | solution.py:58
  77.3 11.9 %fusion.64 = (bf16[4,8,128,1024]{3,2,1,0:T(8,128)(2,1)}, bf16[4,8,128,1024]{3,2,1,0:T(8,128)(2,1)}) fusion(bf16[4,8,128,2048]{3,2,1,0:T(8,128)(2,1)} %bitcast.67), kind=kLoop, calls=%fused_computation.90 | loop fusion | bytes 33554432 | tf_op jit(solution)/shard_map/slice | solution.py:59
  89.2 12.3 %copy.22 = bf16[4,8,128,1024]{2,1,3,0:T(8,128)(2,1)} copy(bf16[4,8,128,1024]{3,2,1,0:T(8,128)(2,1)} %get-tuple-element.6) | data formatting | bytes 16777216 | tf_op jit(solution)/shard_map/slice | solution.py:60
  101.5 13.3 %reshape.62 = bf16[4,1024,16,64]{1,3,2,0:T(8,128)(2,1)} reshape(bf16[4,8,128,1024]{2,1,3,0:T(8,128)(2,1)} %copy.22) | data formatting | bytes 16777216 | tf_op jit(solution)/shard_map/reshape | solution.py:60
  114.8 12.4 %copy.23 = bf16[4,8,128,1024]{2,1,3,0:T(8,128)(2,1)} copy(bf16[4,8,128,1024]{3,2,1,0:T(8,128)(2,1)} %get-tuple-element.5) | data formatting | bytes 16777216 | tf_op jit(solution)/shard_map/slice | solution.py:59
  127.2 13.3 %reshape.63 = bf16[4,1024,16,64]{1,3,2,0:T(8,128)(2,1)} reshape(bf16[4,8,128,1024]{2,1,3,0:T(8,128)(2,1)} %copy.23) | data formatting | bytes 16777216 | tf_op jit(solution)/shard_map/reshape | solution.py:59
  140.5 18.8 %fusion.65 = (f32[4,16,128]{2,1,0:T(8,128)S(1)}, f32[4,16,128,1024]{2,3,1,0:T(8,128)}) fusion(pred[4,1024]{1,0:T(4,128)(4,1)S(1)} %bitcast.69, bf16[4,1024,16,64]{1,3,2,0:T(8,128)(2,1)} %reshape.63, bf16[4,128,16,64]{3,2,1,0:T(8,128)(2,1)} %reshape.79), kind=kOutput, calls=%fused_computation.91 | convolution fusion | flops 1107297280 | bytes 43028480 | tf_op jit(solution)/shard_map/sub | solution.py:69
  159.3 14.7 %fusion.45 = bf16[4,128,16,64]{1,3,2,0:T(8,128)(2,1)S(1)} fusion(bf16[4,1024,16,64]{1,3,2,0:T(8,128)(2,1)} %reshape.62, f32[4,16,128,1024]{2,3,1,0:T(8,128)} %get-tuple-element.8, f32[4,16,128]{2,1,0:T(8,128)S(1)} %get-tuple-element.7), kind=kOutput, calls=%fused_computation.45 | convolution fusion | flops 1091043328 | bytes 43024384 | tf_op jit(solution)/shard_map/thqk,tkhd->tqhd/dot_general | solution.py:71
  173.9 0.0 copy-start.4
  174.0 0.9 copy.27
  174.8 0.0 slice-start
  174.9 0.0 copy-done
  174.9 2.8 multiply_reduce_fusion
  177.6 0.0 copy-start.1
  177.7 1.3 copy-done.1
  179.0 0.0 copy-done.4
  179.0 0.0 slice-start.1
  179.0 0.0 slice-start.2
  179.0 1.4 convert_bitcast_fusion.1
  180.4 35.8 %all_to_all.8 = bf16[128,1,8,1024]{3,2,1,0:T(8,128)(2,1)S(1)} all-to-all(bf16[128,1,8,1024]{3,2,1,0:T(8,128)(2,1)S(1)} %convert_bitcast_fusion.1), channel_id=1, replica_groups=mesh['node'=16,'expert'=8] {'node','expert'}, dimensions={0} | all-to-all | bytes 4194304 | tf_op jit(solution)/shard_map/all_to_all | solution.py:89
  216.2 0.0 slice-done
  216.2 0.0 slice-done.1
  216.2 0.0 slice-start.3
  216.2 11.6 %fusion.19 = f32[1024,4096]{1,0:T(8,128)} fusion(bf16[1,1024,4096]{2,1,0:T(8,128)(2,1)S(1)} %bitcast.71, bf16[128,1,8,1024]{3,2,1,0:T(8,128)(2,1)S(1)} %all_to_all.8), kind=kOutput, calls=%fused_computation.23 | convolution fusion | flops 8589934592 | bytes 27262976 | tf_op jit(solution)/shard_map/dot_general | solution.py:97
  227.8 0.0 slice-done.2
  227.8 0.0 slice-done.3
  227.8 0.0 copy-start.2
  227.8 0.0 copy-start.3
  227.8 14.7 %convert_bitcast_fusion = bf16[1,128,8,1024]{3,2,0,1:T(8,128)(2,1)} fusion(bf16[1,4096,1024]{2,1,0:T(8,128)(2,1)S(1)} %bitcast.73, f32[1024,4096]{1,0:T(8,128)} %fusion.19), kind=kOutput, calls=%fused_computation.34 | convolution fusion | flops 8628731904 | bytes 27262976 | tf_op jit(solution)/shard_map/dot_general | solution.py:99
  242.6 5.8 %all-to-all-start.1 = ((bf16[1,128,8,1024]{3,2,0,1:T(8,128)(2,1)}), bf16[1,128,8,1024]{3,2,0,1:T(8,128)(2,1)}, u32[]{:S(2)}, u32[]{:S(2)}) async-start(bf16[1,128,8,1024]{3,2,0,1:T(8,128)(2,1)} %convert_bitcast_fusion), calls=%async_computation.1 | async-start | bytes 4194304 | tf_op jit(solution)/shard_map/all_to_all | solution.py:100
  248.4 0.0 copy-done.2
  248.4 0.0 copy-done.3
  248.4 2.2 fusion.46
  250.6 27.7 %all-to-all-done.1 = bf16[1,128,8,1024]{3,2,0,1:T(8,128)(2,1)} async-done(((bf16[1,128,8,1024]{3,2,0,1:T(8,128)(2,1)}), bf16[1,128,8,1024]{3,2,0,1:T(8,128)(2,1)}, u32[]{:S(2)}, u32[]{:S(2)}) %all-to-all-start.1) | async-done | bytes 2097184 | tf_op jit(solution)/shard_map/all_to_all | solution.py:100
  278.2 4.5 %add_convert_fusion = bf16[512,1024]{1,0:T(8,128)(2,1)} fusion(f32[512,1024]{1,0:T(8,128)} %copy-done.1, bf16[1,128,8,1024]{3,2,0,1:T(8,128)(2,1)} %all-to-all-done.1, s32[512]{0:T(512)S(1)} %multiply_add_fusion, f32[512]{0:T(512)S(1)} %add_divide_fusion), kind=kOutput, calls=%fused_computation.33 | convolution fusion | flops 1075838976 | bytes 5246976 | tf_op jit(solution)/shard_map/ct,cd->td/dot_general | solution.py:104
  (6 shorter events, 0.0 us)
Async XLA Ops:
  0.0 174.9 %copy-start = (bf16[1024,1024]{1,0:T(8,128)(2,1)S(1)}, bf16[1024,1024]{1,0:T(8,128)(2,1)}, u32[]{:S(2)}) copy-start(bf16[1024,1024]{1,0:T(8,128)(2,1)} %param.19) | copy-start | bytes 6291460
  4.8 51.4 %collective-permute-start.1 = (bf16[512,2048]{1,0:T(8,128)(2,1)}, bf16[512,2048]{1,0:T(8,128)(2,1)}, u32[]{:S(2)}, u32[]{:S(2)}) collective-permute-start(bf16[512,2048]{1,0:T(8,128)(2,1)} %constant_dynamic-update-slice_fusion), channel_id=1, source_target_pairs={{8,0},{16,8},{24,16},{32,24},{40,32},{48,40},{56,48},{64,56},{72,6... | collective-permute-start | bytes 6291464 | tf_op jit(solution)/shard_map/ppermute | solution.py:24
  11.5 49.9 %collective-permute-start = (bf16[512,2048]{1,0:T(8,128)(2,1)}, bf16[512,2048]{1,0:T(8,128)(2,1)}, u32[]{:S(2)}, u32[]{:S(2)}) collective-permute-start(bf16[512,2048]{1,0:T(8,128)(2,1)} %constant_dynamic-update-slice_fusion), channel_id=1, source_target_pairs={{0,8},{8,16},{16,24},{24,32},{32,40},{40,48},{48,56},{56,64},{64,7... | collective-permute-start | bytes 6291464 | tf_op jit(solution)/shard_map/ppermute | solution.py:23
  173.9 5.0 %copy-start.4 = (f32[1024]{0:T(1024)S(1)}, f32[1024]{0:T(1024)}, u32[]{:S(2)}) copy-start(f32[1024]{0:T(1024)} %param.20) | copy-start | bytes 12292
  174.8 41.3 %slice-start = ((s8[8388608]{0:T(1024)(128)(4,1)}), s8[4194304]{0:T(1024)(128)(4,1)S(1)}, s32[]{:S(2)}) async-start(s8[8388608]{0:T(1024)(128)(4,1)} %bitcast.70), calls=%async_computation.2 | async-start | bytes 8388608
  177.6 1.3 copy-start.1
  179.0 37.2 %slice-start.1 = ((s8[8388608]{0:T(1024)(128)(4,1)}), s8[4194304]{0:T(1024)(128)(4,1)S(1)}, s32[]{:S(2)}) async-start(s8[8388608]{0:T(1024)(128)(4,1)} %bitcast.70), calls=%async_computation.3 | async-start | bytes 8388608
  179.0 48.8 %slice-start.2 = ((s8[8388608]{0:T(1024)(128)(4,1)}), s8[4194304]{0:T(1024)(128)(4,1)S(1)}, s32[]{:S(2)}) async-start(s8[8388608]{0:T(1024)(128)(4,1)} %bitcast.72), calls=%async_computation.4 | async-start | bytes 8388608
  216.2 11.7 %slice-start.3 = ((s8[8388608]{0:T(1024)(128)(4,1)}), s8[4194304]{0:T(1024)(128)(4,1)S(1)}, s32[]{:S(2)}) async-start(s8[8388608]{0:T(1024)(128)(4,1)} %bitcast.72), calls=%async_computation.5 | async-start | bytes 8388608
  227.8 20.5 %copy-start.2 = (bf16[1024,128]{1,0:T(8,128)(2,1)S(1)}, bf16[1024,128]{1,0:T(8,128)(2,1)}, u32[]{:S(2)}) copy-start(bf16[1024,128]{1,0:T(8,128)(2,1)} %param.21) | copy-start | bytes 786436
  227.8 20.5 %copy-start.3 = (s32[512]{0:T(512)S(1)}, s32[512]{0:T(512)}, u32[]{:S(2)}) copy-start(s32[512]{0:T(512)} %param.22) | copy-start | bytes 6148
  242.6 35.7 %all-to-all-start.1 = ((bf16[1,128,8,1024]{3,2,0,1:T(8,128)(2,1)}), bf16[1,128,8,1024]{3,2,0,1:T(8,128)(2,1)}, u32[]{:S(2)}, u32[]{:S(2)}) async-start(bf16[1,128,8,1024]{3,2,0,1:T(8,128)(2,1)} %convert_bitcast_fusion), calls=%async_computation.1 | async-start | bytes 4194304 | tf_op jit(solution)/shard_map/all_to_all | solution.py:100
where the time goes:
time: 284 us; the launch traced here: 283 us
  local copies, waits for them, and re-layouts  84.4 us (30%)
  waiting for transfers between devices  71.2 us (25%)
  matrix products  70.6 us (25%)
  blocking collectives  35.8 us (13%)
  starting transfers between devices  12.6 us (4%)
  other arithmetic  8.02 us (3%)
    ppermute x1, waiting for transfers between devices, extended(): after = lax.ppermute(leading, axis, down)  38.3 us
    all_to_all x1, blocking collectives, shards(): lax.all_to_all(outgoing.reshape(experts, 1, cap, D), ('node', 'expert'),...  35.8 us
    all_to_all x1, waiting for transfers between devices, shards(): lax.all_to_all(result.reshape(block.shape), ('node', 'expert'), split_axi...  27.7 us
    slice x2, local copies, waits for them, and re-layouts, shards(): near_keys = gathered[..., :D].reshape(tiles_dev, NB * TILE, HEADS, HEAD_DIM)  24.2 us
    sub x1, matrix products, shards(): weights = jnp.exp(masked - peak)  18.8 us
    dot_general x1, matrix products, shards(): jnp.dot(lifted, down_matrix, preferred_element_type=jnp.float32)  14.7 us
    dot_general x1, matrix products, shards(): jnp.einsum('thqk,tkhd->tqhd', weights, near_values, preferred_element_typ...  14.7 us
    reshape x1, local copies, waits for them, and re-layouts, shards(): gathered[..., D:].reshape(tiles_dev, NB * TILE, HEADS, HEAD_DIM)  13.3 us
  transfers between devices with their start and end apart: 3, of which 3 were waited for; matrix products, arithmetic and copies ran while one was open for 3% of the time, Pallas kernels for 0%

commit v1 on v0

v1 whole, which is shorter than its diff:
```python
import functools

import jax
import jax.numpy as jnp
from jax import lax
from jax.experimental import pallas as pl
from jax.experimental.pallas import tpu as pltpu
from jax.sharding import PartitionSpec as P

MESH = pl.DeviceIdType.MESH
D = 1024
HEADS = 16
HEAD_DIM = 64
FF = 4096
TILE = 128
NB = 8
TOK = 512
TILES = TOK // TILE
CAP = 8
DEVICES = 128
N_NODE = 16
N_EXPERT = 8
LANES = 128
CHUNKS = D // LANES
PARTS = 4
PART_DEVICES = DEVICES // PARTS
PART_ROWS = PART_DEVICES * CAP
FF_BLOCK = 512
OUT_BLOCK = 256
SCALE = 0.125 * 1.4426950408889634
GELU_A = 0.7978845608028654
GELU_B = 0.044715 * GELU_A


def gelu(v):
    return (0.5 * v) * (1.0 + jnp.tanh(v * (GELU_A + GELU_B * (v * v))))


def offset_of(part, i):
    core = i % 2
    z = (i // 2) % 4
    x = i // 8
    y = (part + z + x) % 4
    return z, x, y, core


def kernel(
    nbr_ref, live_ref, tok_hbm, q_hbm, k_hbm, v_hbm, wo_hbm, gain_ref, router_ref, expert_ref, slot_ref, up_hbm, down_hbm,
    out_hbm,
    kv, q_v, tok_v, wo_v, attn_v, near_k, near_v, hidden_v, normed_v, gate_v, col_v,
    send_v, recv_v, res_v, ret_v, up_v, down_v, lifted_v, acc_v, out_v,
    load_sem, kv_sem, q_sem, w_sem, halo_send, halo_recv, disp_send, disp_recv, ret_send, ret_recv, self_sem, out_sem,
):
    node = lax.axis_index("node")
    column = lax.axis_index("expert")
    z, x, y, core = node // 4, node % 4, column // 2, column % 2

    def device(dz, dx, dy, dc):
        return ((z + dz) % 4 * 4 + (x + dx) % 4, (y + dy) % 4 * 2 + (core + dc) % 2)

    barrier = pltpu.get_barrier_semaphore()

    def greet(i, carry):
        pl.semaphore_signal(
            barrier, inc=1, device_id=((node + i // N_EXPERT) % N_NODE, (column + i % N_EXPERT) % N_EXPERT), device_id_type=MESH
        )
        return carry

    lax.fori_loop(1, DEVICES, greet, 0)

    def kv_load(c, which):
        source = k_hbm if which == 0 else v_hbm
        return pltpu.make_async_copy(
            source.at[:, pl.ds(pl.multiple_of(c * LANES, LANES), LANES)], kv.at[0, c, which], kv_sem.at[c, which]
        )

    def start_kv(c, carry):
        kv_load(c, 0).start()
        kv_load(c, 1).start()
        return carry

    lax.fori_loop(0, CHUNKS, start_kv, 0)

    def q_load(c):
        return pltpu.make_async_copy(
            q_hbm.at[:, pl.ds(pl.multiple_of(c * LANES, LANES), LANES)], q_v.at[c], q_sem.at[c]
        )

    def start_q(c, carry):
        q_load(c).start()
        return carry

    lax.fori_loop(0, CHUNKS, start_q, 0)
    tok_load = pltpu.make_async_copy(tok_hbm, tok_v, load_sem.at[0])
    wo_load = pltpu.make_async_copy(wo_hbm, wo_v, load_sem.at[1])
    up_load = pltpu.make_async_copy(up_hbm.at[0], up_v, w_sem.at[0])
    down_load = pltpu.make_async_copy(down_hbm.at[0], down_v, w_sem.at[1])

    pl.semaphore_wait(barrier, DEVICES - 1)

    after = ((node + 1) % N_NODE, column)
    before = ((node + N_NODE - 1) % N_NODE, column)

    def halo(c, side):
        return pltpu.make_async_remote_copy(
            src_ref=kv.at[0, c], dst_ref=kv.at[1 + side, c], send_sem=halo_send.at[side, c], recv_sem=halo_recv.at[side, c],
            device_id=after if side == 0 else before, device_id_type=MESH,
        )

    def start_halo(c, carry):
        kv_load(c, 0).wait()
        kv_load(c, 1).wait()
        halo(c, 0).start()
        halo(c, 1).start()
        return carry

    lax.fori_loop(0, CHUNKS, start_halo, 0)
    tok_load.start()
    wo_load.start()
    up_load.start()
    down_load.start()

    lane = lax.broadcasted_iota(jnp.int32, (TILE, LANES), 1)
    left = lane < HEAD_DIM
    left_mask = jnp.where(left, 1.0, 0.0).astype(jnp.bfloat16)
    right_mask = jnp.where(left, 0.0, 1.0).astype(jnp.bfloat16)

    def attend(c, carry):
        halo(c, 0).wait_recv()
        halo(c, 1).wait_recv()
        q_load(c).wait()
        for b in range(3):
            near_k[pl.ds(b * TILES, TILES)] = kv[b, c, 0].reshape(TILES, TILE, LANES)
            near_v[pl.ds(b * TILES, TILES)] = kv[b, c, 1].reshape(TILES, TILE, LANES)
        for t in range(TILES):
            own = nbr_ref[t, 0] % TILES
            key_tiles = []
            value_tiles = []
            for j in range(NB):
                listed = nbr_ref[t, j]
                step = (listed // (TILES * N_EXPERT) - node + N_NODE) % N_NODE
                block = jnp.where(step == 0, 0, jnp.where(step == 1, 2, 1))
                bit = live_ref[t, j]
                position = jnp.where(bit > 0, block * TILES + listed % TILES, own)
                key_tiles.append(near_k[position])
                shown = jnp.full((TILE, LANES), jnp.where(bit > 0, 1.0, 0.0), jnp.float32).astype(jnp.bfloat16)
                value_tiles.append(jnp.concatenate([near_v[position] * shown, shown], axis=1))
            near_keys = jnp.concatenate(key_tiles, axis=0)
            near_values = jnp.concatenate(value_tiles, axis=0)
            rows = pl.ds(t * TILE, TILE)
            query = q_v[c, rows, :]
            both = jnp.concatenate([query * left_mask, query * right_mask], axis=0)
            scores = lax.dot_general(both, near_keys, (((1,), (1,)), ((), ())), preferred_element_type=jnp.float32)
            peak = jnp.max(scores, axis=1, keepdims=True)
            weights = jnp.exp2((scores - peak) * SCALE).astype(jnp.bfloat16)
            mixed = jnp.dot(weights, near_values, preferred_element_type=jnp.float32)
            ratio = mixed[:, :LANES] / mixed[:, LANES:]
            attn_v[rows, pl.ds(pl.multiple_of(c * LANES, LANES), LANES)] = jnp.where(
                left, ratio[:TILE], ratio[TILE:]
            ).astype(jnp.bfloat16)
        return carry

    lax.fori_loop(0, CHUNKS, attend, 0)

    tok_load.wait()
    wo_load.wait()

    def project(t, carry):
        rows = pl.ds(pl.multiple_of(t * TILE, TILE), TILE)
        hidden = tok_v[rows, :].astype(jnp.float32) + jnp.dot(attn_v[rows, :], wo_v[...], preferred_element_type=jnp.float32)
        hidden_v[rows, :] = hidden
        spread = jnp.mean(hidden * hidden, axis=1, keepdims=True)
        normed = (hidden * lax.rsqrt(spread + 1e-06) * gain_ref[...]).astype(jnp.bfloat16)
        normed_v[rows, :] = normed
        logits = jnp.dot(normed, router_ref[...], preferred_element_type=jnp.float32)
        chosen_row = jnp.broadcast_to(expert_ref[pl.ds(t, 1), :].astype(jnp.float32), (TILE, LANES))
        chosen = jnp.where(lane.astype(jnp.float32) == chosen_row.T, logits, 0.0)
        gate_v[rows, :] = jnp.broadcast_to(jax.nn.sigmoid(jnp.sum(chosen, axis=1, keepdims=True)), (TILE, LANES))
        return carry

    lax.fori_loop(0, TILES, project, 0)

    owner = expert_ref[...]
    dc = (owner % 2 - core + 2) % 2
    dy = (owner // 2 % 4 - y + 4) % 4
    dx = (owner // 8 % 4 - x + 4) % 4
    dz = (owner // 32 - z + 4) % 4
    part_of = (dy + 8 - dz - dx) % 4
    cell = ((part_of * PART_DEVICES + dx * 8 + dz * 2 + dc) * CAP + slot_ref[...]).astype(jnp.float32)
    for t in range(TILES):
        col_v[pl.ds(t * TILE, TILE), :] = jnp.broadcast_to(cell[t : t + 1, :], (TILE, LANES)).T
    cell_row = jnp.concatenate([cell[t : t + 1, :] for t in range(TILES)], axis=1)

    def dispatch(part, i):
        oz, ox, oy, oc = offset_of(part, i)
        at = part * PART_DEVICES + i
        return pltpu.make_async_remote_copy(
            src_ref=send_v.at[at], dst_ref=recv_v.at[at], send_sem=disp_send.at[part], recv_sem=disp_recv.at[part],
            device_id=device(oz, ox, oy, oc), device_id_type=MESH,
        )

    own_copy = pltpu.make_async_copy(send_v.at[0], recv_v.at[0], self_sem.at[0])
    for part in range(PARTS):
        wanted = lax.broadcasted_iota(jnp.int32, (PART_ROWS, TOK), 0).astype(jnp.float32) + part * PART_ROWS
        one_hot = jnp.where(wanted == cell_row, 1.0, 0.0).astype(jnp.bfloat16)
        rows = jnp.dot(one_hot, normed_v[...], preferred_element_type=jnp.float32).astype(jnp.bfloat16)
        send_v[pl.ds(part * PART_DEVICES, PART_DEVICES)] = rows.reshape(PART_DEVICES, CAP, D)

        def start_dispatch(i, carry, part=part):
            dispatch(part, i).start()
            return carry

        lax.fori_loop(1 if part == 0 else 0, PART_DEVICES, start_dispatch, 0)
        if part == 0:
            own_copy.start()

    up_load.wait()
    down_load.wait()

    def give_back(part, i):
        oz, ox, oy, oc = offset_of(part, i)
        at = part * PART_DEVICES + i
        return pltpu.make_async_remote_copy(
            src_ref=res_v.at[at], dst_ref=ret_v.at[at], send_sem=ret_send.at[part], recv_sem=ret_recv.at[part],
            device_id=device(4 - oz, 4 - ox, 4 - oy, 2 - oc), device_id_type=MESH,
        )

    own_back = pltpu.make_async_copy(res_v.at[0], ret_v.at[0], self_sem.at[1])

    def part_slice(part):
        first = part * PART_DEVICES + (1 if part == 0 else 0)
        return pl.ds(first, PART_DEVICES - (1 if part == 0 else 0))

    for part in range(PARTS):
        if part == 0:
            own_copy.wait()
        pltpu.make_async_copy(recv_v.at[part_slice(part)], recv_v.at[part_slice(part)], disp_recv.at[part]).wait()
        here = pl.ds(part * PART_DEVICES, PART_DEVICES)

        def lift(f, carry):
            columns = pl.ds(pl.multiple_of(f * FF_BLOCK, FF_BLOCK), FF_BLOCK)
            rows = recv_v[here].reshape(PART_ROWS, D)
            lifted_v[:, columns] = gelu(
                jnp.dot(rows, up_v[:, columns], preferred_element_type=jnp.float32)
            ).astype(jnp.bfloat16)
            return carry

        lax.fori_loop(0, FF // FF_BLOCK, lift, 0)

        def lower(n, carry):
            columns = pl.ds(pl.multiple_of(n * OUT_BLOCK, OUT_BLOCK), OUT_BLOCK)
            lowered = jnp.dot(lifted_v[...], down_v[:, columns], preferred_element_type=jnp.float32)
            res_v[here, :, columns] = lowered.astype(jnp.bfloat16).reshape(PART_DEVICES, CAP, OUT_BLOCK)
            return carry

        lax.fori_loop(0, D // OUT_BLOCK, lower, 0)

        def start_back(i, carry, part=part):
            give_back(part, i).start()
            return carry

        lax.fori_loop(1 if part == 0 else 0, PART_DEVICES, start_back, 0)
        if part == 0:
            own_back.start()

    for part in range(PARTS):
        if part == 0:
            own_back.wait()
        pltpu.make_async_copy(ret_v.at[part_slice(part)], ret_v.at[part_slice(part)], ret_recv.at[part]).wait()
        here = pl.ds(part * PART_DEVICES, PART_DEVICES)
        for t in range(TILES):
            rows = pl.ds(t * TILE, TILE)
            place = col_v[rows, :]
            one_hot = jnp.concatenate(
                [
                    jnp.where(place == lane.astype(jnp.float32) + (part * PART_ROWS + s * LANES), 1.0, 0.0).astype(jnp.bfloat16)
                    for s in range(PART_ROWS // LANES)
                ],
                axis=1,
            )
            taken = jnp.dot(one_hot, ret_v[here].reshape(PART_ROWS, D), preferred_element_type=jnp.float32)
            if part == 0:
                acc_v[rows, :] = taken
            elif part < PARTS - 1:
                acc_v[rows, :] += taken
            else:
                gate = gate_v[rows, :1]
                out_v[rows, :] = (hidden_v[rows, :] + gate * (acc_v[rows, :] + taken)).astype(jnp.bfloat16)

    store = pltpu.make_async_copy(out_v, out_hbm, out_sem)
    store.start()

    def end_halo(c, carry):
        halo(c, 0).wait_send()
        halo(c, 1).wait_send()
        return carry

    lax.fori_loop(0, CHUNKS, end_halo, 0)
    for part in range(PARTS):
        pltpu.make_async_copy(send_v.at[part_slice(part)], send_v.at[part_slice(part)], disp_send.at[part]).wait()
        pltpu.make_async_copy(res_v.at[part_slice(part)], res_v.at[part_slice(part)], ret_send.at[part]).wait()
    store.wait()


def shards(tokens, queries, keys, values, neighbours, live_bits, out_proj, norm_gain, router, expert, slot, w_up, w_down):
    any_spec = pl.BlockSpec(memory_space=pltpu.HBM)
    smem = pl.BlockSpec(memory_space=pltpu.SMEM)
    vmem = pl.BlockSpec(memory_space=pltpu.VMEM)
    bf16, f32 = jnp.bfloat16, jnp.float32
    dma = pltpu.SemaphoreType.DMA
    return pl.pallas_call(
        kernel,
        name="layer",
        out_shape=jax.ShapeDtypeStruct((TOK, D), bf16),
        in_specs=[smem, smem] + [any_spec] * 5 + [vmem] * 4 + [any_spec] * 2,
        out_specs=any_spec,
        scratch_shapes=[
            pltpu.VMEM((3, CHUNKS, 2, TOK, LANES), bf16),
            pltpu.VMEM((CHUNKS, TOK, LANES), bf16),
            pltpu.VMEM((TOK, D), bf16),
            pltpu.VMEM((D, D), bf16),
            pltpu.VMEM((TOK, D), bf16),
            pltpu.VMEM((3 * TILES, TILE, LANES), bf16),
            pltpu.VMEM((3 * TILES, TILE, LANES), bf16),
            pltpu.VMEM((TOK, D), f32),
            pltpu.VMEM((TOK, D), bf16),
            pltpu.VMEM((TOK, LANES), f32),
            pltpu.VMEM((TOK, LANES), f32),
            pltpu.VMEM((DEVICES, CAP, D), bf16),
            pltpu.VMEM((DEVICES, CAP, D), bf16),
            pltpu.VMEM((DEVICES, CAP, D), bf16),
            pltpu.VMEM((DEVICES, CAP, D), bf16),
            pltpu.VMEM((D, FF), bf16),
            pltpu.VMEM((FF, D), bf16),
            pltpu.VMEM((PART_ROWS, FF), bf16),
            pltpu.VMEM((TOK, D), f32),
            pltpu.VMEM((TOK, D), bf16),
            dma((2,)),
            dma((CHUNKS, 2)),
            dma((CHUNKS,)),
            dma((2,)),
            dma((2, CHUNKS)),
            dma((2, CHUNKS)),
            dma((PARTS,)),
            dma((PARTS,)),
            dma((PARTS,)),
            dma((PARTS,)),
            dma((2,)),
            dma,
        ],
        compiler_params=pltpu.CompilerParams(collective_id=0, has_side_effects=True, vmem_limit_bytes=64_000_000),
    )(
        neighbours, live_bits, tokens, queries, keys, values, out_proj, norm_gain.reshape(1, D), router,
        expert.reshape(TILES, TILE), slot.reshape(TILES, TILE), w_up, w_down,
    )


def solution(mesh):
    rows = P(("node", "expert"), None)
    flat = P(("node", "expert"))
    deep = P(("node", "expert"), None, None)
    in_specs = (rows, rows, rows, rows, rows, rows, P(), P(), P(), flat, flat, deep, deep)
    return jax.shard_map(shards, mesh=mesh, in_specs=in_specs, out_specs=rows, check_vma=False)
```

time: 284 us -> 124 us (0.44)
  Pallas kernels: 0 us -> 122 us
  local copies, waits for them, and re-layouts: 84.4 us -> 2.26 us
  waiting for transfers between devices: 71.2 us -> 0 us
  matrix products: 70.6 us -> 0 us
  blocking collectives: 35.8 us -> 0 us
  starting transfers between devices: 12.6 us -> 0 us
  other arithmetic: 8.02 us -> 0 us
    pallas_call x0 -> x1, Pallas kernels: none -> 122 us  [shards(): pl.pallas_call(kernel, name='layer', out_shape=jax.ShapeDtypeStruct((TOK,...]
    dot_general x7 -> x0, matrix products: 51.8 us -> none  [the longest x1 14.7 us: shards(): jnp.dot(lifted, down_matrix, preferred_element_type=jnp.float32)]
    ppermute x2 -> x0, waiting for transfers between devices: 43.5 us -> none  [the longest x1 38.3 us: extended(): after = lax.ppermute(leading, axis, down)]
    slice x3 -> x0, local copies, waits for them, and re-layouts: 36.5 us -> none  [the longest x2 24.2 us: shards(): near_keys = gathered[..., :D].reshape(tiles_dev, NB * TILE, HEADS, HEAD_DIM)]
    all_to_all x1 -> x0, blocking collectives: 35.8 us -> none  [shards(): lax.all_to_all(outgoing.reshape(experts, 1, cap, D), ('node', 'expert'),...]
    reshape x3 -> x0, local copies, waits for them, and re-layouts: 30.6 us -> none  [the longest x1 13.3 us: shards(): gathered[..., D:].reshape(tiles_dev, NB * TILE, HEADS, HEAD_DIM)]
    all_to_all x1 -> x0, waiting for transfers between devices: 27.7 us -> none  [shards(): lax.all_to_all(result.reshape(block.shape), ('node', 'expert'), split_axi...]
    sub x1 -> x0, matrix products: 18.8 us -> none  [shards(): weights = jnp.exp(masked - peak)]
  transfers between devices with their start and end apart: 3 -> 0, of which waited for: 3 -> 0; matrix products, arithmetic and copies ran while one was open for 3% -> 0% of each run, Pallas kernels for 0% -> 0%
where the time goes in v1:
time: 124 us
  Pallas kernels  122 us (98%)
  local copies, waits for them, and re-layouts  2.26 us (2%)
    pallas_call x1, Pallas kernels, shards(): pl.pallas_call(kernel, name='layer', out_shape=jax.ShapeDtypeStruct((TOK,...  122 us

profile of v1, /device:TPU:1, one launch (start us, length us, event | category | flops | bytes accessed | tf_op | source)
XLA Modules:
  0.0 123.9 jit_solution(1602751822294706805)
XLA Ops:
  0.0 121.7 %layer.1 = bf16[512,1024]{1,0:T(8,128)(2,1)} custom-call(s32[4,8]{1,0:T(4,128)} %nbr_ref.1, s32[4,8]{1,0:T(4,128)} %live_ref.1, bf16[512,1024]{1,0:T(8,128)(2,1)} %tok_hbm.1, bf16[512,1024]{1,0:T(8,128)(2,1)} %q_hbm.1, bf16[512,1024]{1,0:T(8,128)(2,1)} %k_hbm.1, bf16[512,1024]{1,0:T(8,128)(2,1)} %v_hbm.1, bf16[1024,1024]{1,0:T(8,128)(2,1)} %wo_hbm.1, ...), custom_call_target="tpu_custom_call" | custom-call | tf_op jit(solution)/shard_map/layer/pallas_call | solution.py:311
  121.7 2.3 %copy.15 = bf16[512,1024]{1,0:T(8,128)(2,1)} copy(bf16[512,1024]{1,0:T(8,128)(2,1)} %layer.1) | data formatting | bytes 2097152

commit v2 on v1

v2 whole, which is shorter than its diff:
```python
import functools

import jax
import jax.numpy as jnp
from jax import lax
from jax.experimental import pallas as pl
from jax.experimental.pallas import tpu as pltpu
from jax.sharding import PartitionSpec as P

MESH = pl.DeviceIdType.MESH
D = 1024
HEADS = 16
HEAD_DIM = 64
FF = 4096
TILE = 128
NB = 8
TOK = 512
TILES = TOK // TILE
CAP = 8
DEVICES = 128
N_NODE = 16
N_EXPERT = 8
LANES = 128
CHUNKS = D // LANES
PARTS = 4
PART_DEVICES = DEVICES // PARTS
PART_ROWS = PART_DEVICES * CAP
FF_BLOCK = 1024
OUT_BLOCK = 512
VMEM_LIMIT = 58_000_000
SCALE = 0.125 * 1.4426950408889634
GELU_A = 0.7978845608028654
GELU_B = 0.044715 * GELU_A


def gelu(v):
    return (0.5 * v) * (1.0 + jnp.tanh(v * (GELU_A + GELU_B * (v * v))))


def offset_of(part, i):
    core = i % 2
    z = (i // 2) % 4
    x = i // 8
    return z, x, z + x, core


def kernel(
    nbr_hbm, live_hbm, tok_hbm, q_hbm, k_hbm, v_hbm, wo_hbm, gain_hbm, router_hbm, expert_hbm, slot_hbm, up_hbm, down_hbm,
    out_ref,
    nbr_ref, live_ref, gain_v, router_v, expert_v, slot_v,
    kv, q_v, tok_v, wo_v, attn_v, near_k, near_v, weights_v, hidden_v, normed_v, gate_v, col_v,
    send_v, recv_v, res_v, ret_v, up_v, down_v, lifted_v, acc_v,
    load_sem, kv_sem, q_sem, halo_send, halo_recv, disp_send, disp_recv, ret_send, ret_recv, row_sem,
):
    node = lax.axis_index("node")
    column = lax.axis_index("expert")
    z, x, y, core = node // 4, node % 4, column // 2, column % 2

    def kv_load(c, which):
        source = k_hbm if which == 0 else v_hbm
        return pltpu.make_async_copy(
            source.at[:, pl.ds(pl.multiple_of(c * LANES, LANES), LANES)], kv.at[0, c, which], kv_sem.at[c, which]
        )

    def start_kv(c, carry):
        kv_load(c, 0).start()
        kv_load(c, 1).start()
        return carry

    lax.fori_loop(0, CHUNKS, start_kv, 0)

    barrier = pltpu.get_barrier_semaphore()
    for step in (1, N_NODE - 1) + tuple(range(2, N_NODE - 1)):
        pl.semaphore_signal(barrier, inc=1, device_id=((node + step) % N_NODE, column), device_id_type=MESH)
    for step in range(1, N_EXPERT):
        pl.semaphore_signal(barrier, inc=1, device_id=(node, (column + step) % N_EXPERT), device_id_type=MESH)

    def q_load(c):
        return pltpu.make_async_copy(
            q_hbm.at[:, pl.ds(pl.multiple_of(c * LANES, LANES), LANES)], q_v.at[c], q_sem.at[c]
        )

    def start_q(c, carry):
        q_load(c).start()
        return carry

    small_loads = [
        pltpu.make_async_copy(source, target, load_sem.at[4 + i])
        for i, (source, target) in enumerate(
            (
                (nbr_hbm, nbr_ref), (live_hbm, live_ref), (gain_hbm, gain_v), (router_hbm, router_v),
                (expert_hbm, expert_v), (slot_hbm, slot_v),
            )
        )
    ]
    tok_load = pltpu.make_async_copy(tok_hbm, tok_v, load_sem.at[0])
    wo_load = pltpu.make_async_copy(wo_hbm, wo_v, load_sem.at[1])
    up_load = pltpu.make_async_copy(up_hbm.at[0], up_v, load_sem.at[2])
    down_load = pltpu.make_async_copy(down_hbm.at[0], down_v, load_sem.at[3])

    pl.semaphore_wait(barrier, N_NODE - 1 + N_EXPERT - 1)

    after = ((node + 1) % N_NODE, column)
    before = ((node + N_NODE - 1) % N_NODE, column)

    def halo(c, which, side):
        return pltpu.make_async_remote_copy(
            src_ref=kv.at[0, c, which], dst_ref=kv.at[1 + side, c, which],
            send_sem=halo_send.at[side, c, which], recv_sem=halo_recv.at[side, c, which],
            device_id=after if side == 0 else before, device_id_type=MESH,
        )

    def start_halo(c, carry):
        for which in range(2):
            kv_load(c, which).wait()
            halo(c, which, 0).start()
            halo(c, which, 1).start()
        return carry

    lax.fori_loop(0, CHUNKS, start_halo, 0)
    for load in small_loads:
        load.start()
    lax.fori_loop(0, CHUNKS, start_q, 0)
    tok_load.start()
    wo_load.start()
    up_load.start()
    down_load.start()

    for step in range(1, N_EXPERT):
        pl.semaphore_signal(row_sem, inc=1, device_id=(node, (column + step) % N_EXPERT), device_id_type=MESH)

    for load in small_loads:
        load.wait()

    owner = expert_v[...]
    dc = (owner % 2 - core + 2) % 2
    dy = (owner // 2 % 4 - y + 4) % 4
    dx = (owner // 8 % 4 - x + 4) % 4
    dz = (owner // 32 - z + 4) % 4
    part_of = (dy + 8 - dz - dx) % 4
    cell = ((part_of * PART_DEVICES + dx * 8 + dz * 2 + dc) * CAP + slot_v[...]).astype(jnp.float32)
    for t in range(TILES):
        col_v[pl.ds(t * TILE, TILE), :] = jnp.broadcast_to(cell[t : t + 1, :], (TILE, LANES)).T

    lane = lax.broadcasted_iota(jnp.int32, (TILE, LANES), 1)
    left = lane < HEAD_DIM
    left_mask = jnp.where(left, 1.0, 0.0).astype(jnp.bfloat16)
    right_mask = jnp.where(left, 0.0, 1.0).astype(jnp.bfloat16)

    tok_load.wait()
    hidden_v[...] = tok_v[...].astype(jnp.float32)
    wo_load.wait()

    def lanes_of(c):
        return pl.ds(pl.multiple_of(c * LANES, LANES), LANES)

    def listed(t, j):
        tile = nbr_ref[t, j]
        step = (tile // (TILES * N_EXPERT) - node + N_NODE) % N_NODE
        block = jnp.where(step == 0, 0, jnp.where(step == 1, 2, 1))
        bit = live_ref[t, j]
        return jnp.where(bit > 0, block * TILES + tile % TILES, nbr_ref[t, 0] % TILES), bit

    def attend(c, carry):
        @pl.when(c > 0)
        def _():
            for t in range(TILES):
                rows = pl.ds(t * TILE, TILE)
                hidden_v[rows, :] += jnp.dot(
                    attn_v[rows, lanes_of(c - 1)], wo_v[lanes_of(c - 1), :], preferred_element_type=jnp.float32
                )

        q_load(c).wait()
        halo(c, 0, 0).wait_recv()
        halo(c, 0, 1).wait_recv()
        for b in range(3):
            near_k[pl.ds(b * TILES, TILES)] = kv[b, c, 0].reshape(TILES, TILE, LANES)
        for t in range(TILES):
            near_keys = jnp.concatenate([near_k[listed(t, j)[0]] for j in range(NB)], axis=0)
            query = q_v[c, pl.ds(t * TILE, TILE), :]
            both = jnp.concatenate([query * left_mask, query * right_mask], axis=0)
            scores = lax.dot_general(both, near_keys, (((1,), (1,)), ((), ())), preferred_element_type=jnp.float32)
            peak = jnp.max(scores, axis=1, keepdims=True)
            weights_v[t] = jnp.exp2((scores - peak) * SCALE).astype(jnp.bfloat16)
        halo(c, 1, 0).wait_recv()
        halo(c, 1, 1).wait_recv()
        for b in range(3):
            near_v[pl.ds(b * TILES, TILES)] = kv[b, c, 1].reshape(TILES, TILE, LANES)
        for t in range(TILES):
            value_tiles = []
            for j in range(NB):
                position, bit = listed(t, j)
                shown = jnp.full((TILE, LANES), jnp.where(bit > 0, 1.0, 0.0), jnp.float32).astype(jnp.bfloat16)
                value_tiles.append(jnp.concatenate([near_v[position] * shown, shown], axis=1))
            mixed = jnp.dot(weights_v[t], jnp.concatenate(value_tiles, axis=0), preferred_element_type=jnp.float32)
            ratio = mixed[:, :LANES] / mixed[:, LANES:]
            attn_v[pl.ds(t * TILE, TILE), lanes_of(c)] = jnp.where(left, ratio[:TILE], ratio[TILE:]).astype(jnp.bfloat16)
        return carry

    lax.fori_loop(0, CHUNKS, attend, 0)

    last = pl.ds((CHUNKS - 1) * LANES, LANES)
    for t in range(TILES):
        rows = pl.ds(t * TILE, TILE)
        hidden = hidden_v[rows, :] + jnp.dot(attn_v[rows, last], wo_v[last, :], preferred_element_type=jnp.float32)
        hidden_v[rows, :] = hidden
        spread = jnp.mean(hidden * hidden, axis=1, keepdims=True)
        normed_v[rows, :] = (hidden * lax.rsqrt(spread + 1e-06) * gain_v[...]).astype(jnp.bfloat16)

    pl.semaphore_wait(row_sem, N_EXPERT - 1)
    up_z = [(z + d) % 4 * 4 for d in range(4)]
    up_x = [(x + d) % 4 for d in range(4)]
    up_core = [(core + d) % 2 for d in range(2)]
    down_z = [(z + 4 - d) % 4 * 4 for d in range(4)]
    down_x = [(x + 4 - d) % 4 for d in range(4)]

    def dispatch(part, i, up_y):
        oz, ox, oy, oc = offset_of(part, i)
        at = part * PART_DEVICES + i
        return pltpu.make_async_remote_copy(
            src_ref=send_v.at[at], dst_ref=recv_v.at[at], send_sem=disp_send.at[part], recv_sem=disp_recv.at[part],
            device_id=(up_z[oz] + up_x[ox], up_y[oy % 4] + up_core[oc]), device_id_type=MESH,
        )

    cell_row = jnp.concatenate([cell[t : t + 1, :] for t in range(TILES)], axis=1)
    for part in range(PARTS):
        wanted = lax.broadcasted_iota(jnp.int32, (PART_ROWS, TOK), 0).astype(jnp.float32) + part * PART_ROWS
        one_hot = jnp.where(wanted == cell_row, 1.0, 0.0).astype(jnp.bfloat16)
        rows = jnp.dot(one_hot, normed_v[...], preferred_element_type=jnp.float32).astype(jnp.bfloat16)
        send_v[pl.ds(part * PART_DEVICES, PART_DEVICES)] = rows.reshape(PART_DEVICES, CAP, D)
        up_y = [(y + part + d) % 4 * 2 for d in range(4)]
        for i in range(PART_DEVICES):
            if part == 0 and i == 0:
                pltpu.make_async_copy(send_v.at[0], recv_v.at[0], disp_recv.at[0]).start()
            else:
                dispatch(part, i, up_y).start()

    for t in range(TILES):
        rows = pl.ds(t * TILE, TILE)
        logits = jnp.dot(normed_v[rows, :], router_v[...], preferred_element_type=jnp.float32)
        chosen_row = jnp.broadcast_to(owner[t : t + 1, :].astype(jnp.float32), (TILE, LANES))
        chosen = jnp.where(lane.astype(jnp.float32) == chosen_row.T, logits, 0.0)
        gate_v[rows, :] = jnp.broadcast_to(jax.nn.sigmoid(jnp.sum(chosen, axis=1, keepdims=True)), (TILE, LANES))

    up_load.wait()
    down_load.wait()

    def part_slots(part):
        return pl.ds(part * PART_DEVICES, PART_DEVICES)

    def serve(part, carry):
        here = part_slots(part)
        pltpu.make_async_copy(recv_v.at[here], recv_v.at[here], disp_recv.at[part]).wait()

        def lift(f, carry):
            columns = pl.ds(pl.multiple_of(f * FF_BLOCK, FF_BLOCK), FF_BLOCK)
            rows = recv_v[here].reshape(PART_ROWS, D)
            lifted_v[:, columns] = gelu(
                jnp.dot(rows, up_v[:, columns], preferred_element_type=jnp.float32)
            ).astype(jnp.bfloat16)
            return carry

        lax.fori_loop(0, FF // FF_BLOCK, lift, 0)

        def lower(n, carry):
            columns = pl.ds(pl.multiple_of(n * OUT_BLOCK, OUT_BLOCK), OUT_BLOCK)
            lowered = jnp.dot(lifted_v[...], down_v[:, columns], preferred_element_type=jnp.float32)
            res_v[here, :, columns] = lowered.astype(jnp.bfloat16).reshape(PART_DEVICES, CAP, OUT_BLOCK)
            return carry

        lax.fori_loop(0, D // OUT_BLOCK, lower, 0)

        down_y = [(y + 8 - part - d) % 4 * 2 for d in range(4)]
        for i in range(PART_DEVICES):
            oz, ox, oy, oc = offset_of(part, i)
            at = part * PART_DEVICES + i
            back = pltpu.make_async_remote_copy(
                src_ref=res_v.at[at], dst_ref=ret_v.at[at], send_sem=ret_send.at[part], recv_sem=ret_recv.at[part],
                device_id=(down_z[oz] + down_x[ox], down_y[oy % 4] + up_core[oc]), device_id_type=MESH,
            )
            if i > 0:
                back.start()
            else:
                pl.when(part > 0)(back.start)
                own = pltpu.make_async_copy(res_v.at[0], ret_v.at[0], ret_recv.at[0])
                pl.when(part == 0)(own.start)
        return carry

    lax.fori_loop(0, PARTS, serve, 0)

    for part in range(PARTS):
        here = part_slots(part)
        pltpu.make_async_copy(ret_v.at[here], ret_v.at[here], ret_recv.at[part]).wait()
        for t in range(TILES):
            rows = pl.ds(t * TILE, TILE)
            place = col_v[rows, :]
            one_hot = jnp.concatenate(
                [
                    jnp.where(place == lane.astype(jnp.float32) + (part * PART_ROWS + s * LANES), 1.0, 0.0).astype(jnp.bfloat16)
                    for s in range(PART_ROWS // LANES)
                ],
                axis=1,
            )
            taken = jnp.dot(one_hot, ret_v[here].reshape(PART_ROWS, D), preferred_element_type=jnp.float32)
            if part == 0:
                acc_v[rows, :] = taken
            elif part < PARTS - 1:
                acc_v[rows, :] += taken
            else:
                gate = gate_v[rows, :1]
                out_ref[rows, :] = (hidden_v[rows, :] + gate * (acc_v[rows, :] + taken)).astype(jnp.bfloat16)

    def end_halo(c, carry):
        for which in range(2):
            halo(c, which, 0).wait_send()
            halo(c, which, 1).wait_send()
        return carry

    lax.fori_loop(0, CHUNKS, end_halo, 0)
    for part in range(PARTS):
        sent = pl.ds(part * PART_DEVICES + (1 if part == 0 else 0), PART_DEVICES - (1 if part == 0 else 0))
        pltpu.make_async_copy(send_v.at[sent], send_v.at[sent], disp_send.at[part]).wait()
        pltpu.make_async_copy(res_v.at[sent], res_v.at[sent], ret_send.at[part]).wait()


def shards(tokens, queries, keys, values, neighbours, live_bits, out_proj, norm_gain, router, expert, slot, w_up, w_down):
    hbm = pl.BlockSpec(memory_space=pltpu.HBM)
    bf16, f32 = jnp.bfloat16, jnp.float32
    dma = pltpu.SemaphoreType.DMA
    return pl.pallas_call(
        kernel,
        name="layer",
        out_shape=jax.ShapeDtypeStruct((TOK, D), bf16),
        in_specs=[hbm] * 13,
        out_specs=pl.BlockSpec(memory_space=pltpu.VMEM),
        scratch_shapes=[
            pltpu.SMEM((TILES, NB), jnp.int32),
            pltpu.SMEM((TILES, NB), jnp.int32),
            pltpu.VMEM((1, D), f32),
            pltpu.VMEM((D, LANES), bf16),
            pltpu.VMEM((TILES, TILE), jnp.int32),
            pltpu.VMEM((TILES, TILE), jnp.int32),
            pltpu.VMEM((3, CHUNKS, 2, TOK, LANES), bf16),
            pltpu.VMEM((CHUNKS, TOK, LANES), bf16),
            pltpu.VMEM((TOK, D), bf16),
            pltpu.VMEM((D, D), bf16),
            pltpu.VMEM((TOK, D), bf16),
            pltpu.VMEM((3 * TILES, TILE, LANES), bf16),
            pltpu.VMEM((3 * TILES, TILE, LANES), bf16),
            pltpu.VMEM((TILES, 2 * TILE, NB * TILE), bf16),
            pltpu.VMEM((TOK, D), f32),
            pltpu.VMEM((TOK, D), bf16),
            pltpu.VMEM((TOK, LANES), f32),
            pltpu.VMEM((TOK, LANES), f32),
            pltpu.VMEM((DEVICES, CAP, D), bf16),
            pltpu.VMEM((DEVICES, CAP, D), bf16),
            pltpu.VMEM((DEVICES, CAP, D), bf16),
            pltpu.VMEM((DEVICES, CAP, D), bf16),
            pltpu.VMEM((D, FF), bf16),
            pltpu.VMEM((FF, D), bf16),
            pltpu.VMEM((PART_ROWS, FF), bf16),
            pltpu.VMEM((TOK, D), f32),
            dma((10,)),
            dma((CHUNKS, 2)),
            dma((CHUNKS,)),
            dma((2, CHUNKS, 2)),
            dma((2, CHUNKS, 2)),
            dma((PARTS,)),
            dma((PARTS,)),
            dma((PARTS,)),
            dma((PARTS,)),
            pltpu.SemaphoreType.REGULAR,
        ],
        compiler_params=pltpu.CompilerParams(collective_id=0, has_side_effects=True, vmem_limit_bytes=VMEM_LIMIT),
    )(
        neighbours, live_bits, tokens, queries, keys, values, out_proj, norm_gain.reshape(1, D), router,
        expert.reshape(TILES, TILE), slot.reshape(TILES, TILE), w_up, w_down,
    )


def solution(mesh):
    rows = P(("node", "expert"), None)
    flat = P(("node", "expert"))
    deep = P(("node", "expert"), None, None)
    in_specs = (rows, rows, rows, rows, rows, rows, P(), P(), P(), flat, flat, deep, deep)
    return jax.shard_map(shards, mesh=mesh, in_specs=in_specs, out_specs=rows, check_vma=False)
```

time: 124 us -> 112 us (0.903)
  Pallas kernels: 122 us -> 109 us
    pallas_call x1, Pallas kernels: 122 us -> 109 us  [shards(): pl.pallas_call(kernel, name='layer', out_shape=jax.ShapeDtypeStruct((TOK,...]
where the time goes in v2:
time: 112 us
  Pallas kernels  109 us (97%)
  local copies, waits for them, and re-layouts  2.26 us (2%)
    pallas_call x1, Pallas kernels, shards(): pl.pallas_call(kernel, name='layer', out_shape=jax.ShapeDtypeStruct((TOK,...  109 us
    unnamed x1, local copies, waits for them, and re-layouts  2.26 us

profile of v2, /device:TPU:1, one launch (start us, length us, event | category | flops | bytes accessed | tf_op | source)
XLA Modules:
  0.0 111.6 jit_solution(3051455982082651492)
XLA Ops:
  0.0 109.4 %layer.1 = bf16[512,1024]{1,0:T(8,128)(2,1)} custom-call(s32[4,8]{1,0:T(4,128)} %nbr_hbm.1, s32[4,8]{1,0:T(4,128)} %live_hbm.1, bf16[512,1024]{1,0:T(8,128)(2,1)} %tok_hbm.1, bf16[512,1024]{1,0:T(8,128)(2,1)} %q_hbm.1, bf16[512,1024]{1,0:T(8,128)(2,1)} %k_hbm.1, bf16[512,1024]{1,0:T(8,128)(2,1)} %v_hbm.1, bf16[1024,1024]{1,0:T(8,128)(2,1)} %wo_hbm.1, ...), custom_call_target="tpu_custom_call" | custom-call | tf_op jit(solution)/shard_map/layer/pallas_call | solution.py:330
  109.4 2.3 %copy.15 = bf16[512,1024]{1,0:T(8,128)(2,1)} copy(bf16[512,1024]{1,0:T(8,128)(2,1)} %layer.1) | data formatting | bytes 2097152

commit v3 on v2

--- a/solution.py
+++ b/solution.py
@@ -27,7 +27,7 @@
 PART_ROWS = PART_DEVICES * CAP
 FF_BLOCK = 1024
 OUT_BLOCK = 512
-VMEM_LIMIT = 58_000_000
+VMEM_LIMIT = 56_000_000
 SCALE = 0.125 * 1.4426950408889634
 GELU_A = 0.7978845608028654
 GELU_B = 0.044715 * GELU_A
@@ -49,8 +49,8 @@
     out_ref,
     nbr_ref, live_ref, gain_v, router_v, expert_v, slot_v,
     kv, q_v, tok_v, wo_v, attn_v, near_k, near_v, weights_v, hidden_v, normed_v, gate_v, col_v,
-    send_v, recv_v, res_v, ret_v, up_v, down_v, lifted_v, acc_v,
-    load_sem, kv_sem, q_sem, halo_send, halo_recv, disp_send, disp_recv, ret_send, ret_recv, row_sem,
+    send_v, recv_v, res_v, ret_v, up_v, down_v, lifted_v, acc_v, sum_v,
+    load_sem, kv_sem, q_sem, halo_send, halo_recv, disp_send, disp_recv, ret_send, ret_recv, row_sem, ring_sem,
 ):
     node = lax.axis_index("node")
     column = lax.axis_index("expert")
@@ -70,8 +70,12 @@
     lax.fori_loop(0, CHUNKS, start_kv, 0)
 
     barrier = pltpu.get_barrier_semaphore()
-    for step in (1, N_NODE - 1) + tuple(range(2, N_NODE - 1)):
-        pl.semaphore_signal(barrier, inc=1, device_id=((node + step) % N_NODE, column), device_id_type=MESH)
+
+    def tell_ring(semaphore, step):
+        for peer in (node + step, node + N_NODE - step):
+            pl.semaphore_signal(semaphore, inc=1, device_id=(peer % N_NODE, column), device_id_type=MESH)
+
+    tell_ring(barrier, 1)
     for step in range(1, N_EXPERT):
         pl.semaphore_signal(barrier, inc=1, device_id=(node, (column + step) % N_EXPERT), device_id_type=MESH)
 
@@ -98,7 +102,7 @@
     up_load = pltpu.make_async_copy(up_hbm.at[0], up_v, load_sem.at[2])
     down_load = pltpu.make_async_copy(down_hbm.at[0], down_v, load_sem.at[3])
 
-    pl.semaphore_wait(barrier, N_NODE - 1 + N_EXPERT - 1)
+    pl.semaphore_wait(barrier, 2 + N_EXPERT - 1)
 
     after = ((node + 1) % N_NODE, column)
     before = ((node + N_NODE - 1) % N_NODE, column)
@@ -126,8 +130,15 @@
     up_load.start()
     down_load.start()
 
-    for step in range(1, N_EXPERT):
-        pl.semaphore_signal(row_sem, inc=1, device_id=(node, (column + step) % N_EXPERT), device_id_type=MESH)
+    tell_ring(ring_sem.at[0], 1)
+
+    def spread_word(level):
+        pl.semaphore_wait(ring_sem.at[level], 2)
+        if level < 2:
+            tell_ring(ring_sem.at[level + 1], 2 << level)
+        else:
+            for step in range(1, N_EXPERT):
+                pl.semaphore_signal(row_sem, inc=1, device_id=(node, (column + step) % N_EXPERT), device_id_type=MESH)
 
     for load in small_loads:
         load.wait()
@@ -195,6 +206,8 @@
             mixed = jnp.dot(weights_v[t], jnp.concatenate(value_tiles, axis=0), preferred_element_type=jnp.float32)
             ratio = mixed[:, :LANES] / mixed[:, LANES:]
             attn_v[pl.ds(t * TILE, TILE), lanes_of(c)] = jnp.where(left, ratio[:TILE], ratio[TILE:]).astype(jnp.bfloat16)
+        for level in range(3):
+            pl.when(c == level)(functools.partial(spread_word, level))
         return carry
 
     lax.fori_loop(0, CHUNKS, attend, 0)
@@ -252,23 +265,27 @@
         here = part_slots(part)
         pltpu.make_async_copy(recv_v.at[here], recv_v.at[here], disp_recv.at[part]).wait()
 
-        def lift(f, carry):
-            columns = pl.ds(pl.multiple_of(f * FF_BLOCK, FF_BLOCK), FF_BLOCK)
-            rows = recv_v[here].reshape(PART_ROWS, D)
+        rows = recv_v[here].reshape(PART_ROWS, D)
+        blocks = FF // FF_BLOCK
+
+        def lift(f):
+            columns = slice(f * FF_BLOCK, (f + 1) * FF_BLOCK)
             lifted_v[:, columns] = gelu(
                 jnp.dot(rows, up_v[:, columns], preferred_element_type=jnp.float32)
             ).astype(jnp.bfloat16)
-            return carry
-
-        lax.fori_loop(0, FF // FF_BLOCK, lift, 0)
-
-        def lower(n, carry):
-            columns = pl.ds(pl.multiple_of(n * OUT_BLOCK, OUT_BLOCK), OUT_BLOCK)
-            lowered = jnp.dot(lifted_v[...], down_v[:, columns], preferred_element_type=jnp.float32)
-            res_v[here, :, columns] = lowered.astype(jnp.bfloat16).reshape(PART_DEVICES, CAP, OUT_BLOCK)
-            return carry
-
-        lax.fori_loop(0, D // OUT_BLOCK, lower, 0)
+
+        lift(0)
+        for f in range(1, blocks + 1):
+            inner = slice((f - 1) * FF_BLOCK, f * FF_BLOCK)
+            lowered = jnp.dot(lifted_v[:, inner], down_v[inner, :], preferred_element_type=jnp.float32)
+            if f == 1:
+                sum_v[...] = lowered
+            elif f < blocks:
+                sum_v[...] += lowered
+            else:
+                res_v[here] = (sum_v[...] + lowered).astype(jnp.bfloat16).reshape(PART_DEVICES, CAP, D)
+            if f < blocks:
+                lift(f)
 
         down_y = [(y + 8 - part - d) % 4 * 2 for d in range(4)]
         for i in range(PART_DEVICES):
@@ -330,7 +347,7 @@
     return pl.pallas_call(
         kernel,
         name="layer",
-        out_shape=jax.ShapeDtypeStruct((TOK, D), bf16),
+        out_shape=pltpu.VMEM((TOK, D), bf16),
         in_specs=[hbm] * 13,
         out_specs=pl.BlockSpec(memory_space=pltpu.VMEM),
         scratch_shapes=[
@@ -360,6 +377,7 @@
             pltpu.VMEM((FF, D), bf16),
             pltpu.VMEM((PART_ROWS, FF), bf16),
             pltpu.VMEM((TOK, D), f32),
+            pltpu.VMEM((PART_ROWS, D), f32),
             dma((10,)),
             dma((CHUNKS, 2)),
             dma((CHUNKS,)),
@@ -370,11 +388,17 @@
             dma((PARTS,)),
             dma((PARTS,)),
             pltpu.SemaphoreType.REGULAR,
+            pltpu.SemaphoreType.REGULAR((3,)),
         ],
         compiler_params=pltpu.CompilerParams(collective_id=0, has_side_effects=True, vmem_limit_bytes=VMEM_LIMIT),
     )(
-        neighbours, live_bits, tokens, queries, keys, values, out_proj, norm_gain.reshape(1, D), router,
-        expert.reshape(TILES, TILE), slot.reshape(TILES, TILE), w_up, w_down,
+        *[
+            pltpu.with_memory_space_constraint(array, pltpu.HBM)
+            for array in (
+                neighbours, live_bits, tokens, queries, keys, values, out_proj, norm_gain.reshape(1, D), router,
+                expert.reshape(TILES, TILE), slot.reshape(TILES, TILE), w_up, w_down,
+            )
+        ]
     )
 
 

time: 112 us -> 109 us (0.973)
  Pallas kernels: 109 us -> 107 us
  local copies, waits for them, and re-layouts: 2.26 us -> 0.97 us
    pallas_call x1, Pallas kernels: 109 us -> 107 us  [shards(): pl.pallas_call(kernel, name='layer', out_shape=pltpu.VMEM((TOK, D), bf16)...]
    unnamed x1, local copies, waits for them, and re-layouts: 2.26 us -> 0.97 us
where the time goes in v3:
time: 109 us; the launch traced here: 108 us
  Pallas kernels  107 us (98%)
    pallas_call x1, Pallas kernels, shards(): pl.pallas_call(kernel, name='layer', out_shape=pltpu.VMEM((TOK, D), bf16)...  107 us

profile of v3, /device:TPU:1, one launch (start us, length us, event | category | flops | bytes accessed | tf_op | source)
XLA Modules:
  0.0 108.4 jit_solution(10397125142191793583)
XLA Ops:
  0.0 107.5 %layer.1 = bf16[512,1024]{1,0:T(8,128)(2,1)S(1)} custom-call(s32[4,8]{1,0:T(4,128)} %nbr_hbm.1, s32[4,8]{1,0:T(4,128)} %live_hbm.1, bf16[512,1024]{1,0:T(8,128)(2,1)} %tok_hbm.1, bf16[512,1024]{1,0:T(8,128)(2,1)} %q_hbm.1, bf16[512,1024]{1,0:T(8,128)(2,1)} %k_hbm.1, bf16[512,1024]{1,0:T(8,128)(2,1)} %v_hbm.1, bf16[1024,1024]{1,0:T(8,128)(2,1)} %wo_hbm.1, ...), custom_call_target="tpu_custom_call" | custom-call | tf_op jit(solution)/shard_map/layer/pallas_call | solution.py:347
  107.5 1.0 copy.15

commit v4 on v3

--- a/solution.py
+++ b/solution.py
@@ -38,10 +38,11 @@
 
 
 def offset_of(part, i):
-    core = i % 2
-    z = (i // 2) % 4
-    x = i // 8
-    return z, x, z + x, core
+    core = i // 16
+    z = i % 4
+    x = i // 4 % 4
+    y = z + x
+    return z, x, y, core
 
 
 def kernel(
@@ -149,7 +150,7 @@
     dx = (owner // 8 % 4 - x + 4) % 4
     dz = (owner // 32 - z + 4) % 4
     part_of = (dy + 8 - dz - dx) % 4
-    cell = ((part_of * PART_DEVICES + dx * 8 + dz * 2 + dc) * CAP + slot_v[...]).astype(jnp.float32)
+    cell = ((part_of * PART_DEVICES + dc * 16 + dx * 4 + dz) * CAP + slot_v[...]).astype(jnp.float32)
     for t in range(TILES):
         col_v[pl.ds(t * TILE, TILE), :] = jnp.broadcast_to(cell[t : t + 1, :], (TILE, LANES)).T
 
@@ -223,16 +224,17 @@
     pl.semaphore_wait(row_sem, N_EXPERT - 1)
     up_z = [(z + d) % 4 * 4 for d in range(4)]
     up_x = [(x + d) % 4 for d in range(4)]
+    up_y = [(y + d) % 4 * 2 for d in range(4)]
     up_core = [(core + d) % 2 for d in range(2)]
     down_z = [(z + 4 - d) % 4 * 4 for d in range(4)]
     down_x = [(x + 4 - d) % 4 for d in range(4)]
 
-    def dispatch(part, i, up_y):
+    def dispatch(part, i, up_z, up_x, up_y):
         oz, ox, oy, oc = offset_of(part, i)
         at = part * PART_DEVICES + i
         return pltpu.make_async_remote_copy(
             src_ref=send_v.at[at], dst_ref=recv_v.at[at], send_sem=disp_send.at[part], recv_sem=disp_recv.at[part],
-            device_id=(up_z[oz] + up_x[ox], up_y[oy % 4] + up_core[oc]), device_id_type=MESH,
+            device_id=(up_z[oz % 4] + up_x[ox % 4], up_y[oy % 4] + up_core[oc]), device_id_type=MESH,
         )
 
     cell_row = jnp.concatenate([cell[t : t + 1, :] for t in range(TILES)], axis=1)
@@ -246,7 +248,7 @@
             if part == 0 and i == 0:
                 pltpu.make_async_copy(send_v.at[0], recv_v.at[0], disp_recv.at[0]).start()
             else:
-                dispatch(part, i, up_y).start()
+                dispatch(part, i, up_z, up_x, up_y).start()
 
     for t in range(TILES):
         rows = pl.ds(t * TILE, TILE)
@@ -287,13 +289,15 @@
             if f < blocks:
                 lift(f)
 
+        down_z = [(z + 4 - d) % 4 * 4 for d in range(4)]
+        down_x = [(x + 4 - d) % 4 for d in range(4)]
         down_y = [(y + 8 - part - d) % 4 * 2 for d in range(4)]
         for i in range(PART_DEVICES):
             oz, ox, oy, oc = offset_of(part, i)
             at = part * PART_DEVICES + i
             back = pltpu.make_async_remote_copy(
                 src_ref=res_v.at[at], dst_ref=ret_v.at[at], send_sem=ret_send.at[part], recv_sem=ret_recv.at[part],
-                device_id=(down_z[oz] + down_x[ox], down_y[oy % 4] + up_core[oc]), device_id_type=MESH,
+                device_id=(down_z[oz % 4] + down_x[ox % 4], down_y[oy % 4] + up_core[oc]), device_id_type=MESH,
             )
             if i > 0:
                 back.start()

time: 109 us -> 108 us (level)
  no operation moved by 1% of the time
where the time goes in v4:
time: 108 us
  Pallas kernels  107 us (99%)
    pallas_call x1, Pallas kernels, shards(): pl.pallas_call(kernel, name='layer', out_shape=pltpu.VMEM((TOK, D), bf16)...  107 us

profile of v4, /device:TPU:1, one launch (start us, length us, event | category | flops | bytes accessed | tf_op | source)
XLA Modules:
  0.0 108.1 jit_solution(15574353403074025873)
XLA Ops:
  0.0 107.1 %layer.1 = bf16[512,1024]{1,0:T(8,128)(2,1)S(1)} custom-call(s32[4,8]{1,0:T(4,128)} %nbr_hbm.1, s32[4,8]{1,0:T(4,128)} %live_hbm.1, bf16[512,1024]{1,0:T(8,128)(2,1)} %tok_hbm.1, bf16[512,1024]{1,0:T(8,128)(2,1)} %q_hbm.1, bf16[512,1024]{1,0:T(8,128)(2,1)} %k_hbm.1, bf16[512,1024]{1,0:T(8,128)(2,1)} %v_hbm.1, bf16[1024,1024]{1,0:T(8,128)(2,1)} %wo_hbm.1, ...), custom_call_target="tpu_custom_call" | custom-call | tf_op jit(solution)/shard_map/layer/pallas_call | solution.py:351
  107.1 1.0 copy.15
